TPU v7x, 16 devices: a whole 2x2x2 slice. The times are simulated.
16 devices in a mesh: q: 16 (over z, y, x, core).
Axes of the slice: x: 2, y: 2, z: 2, core: 2. Of those that a mesh axis runs over, the one named last changes fastest.
Arguments:
- state_in: float32 [2, 33554432], P(None, 'q')
- unitaries: float32 [2, 25, 2, 2], replicated
- cz_pairs: int32 [12, 2], replicated
Outputs:
- output 1: float32 [2, 33554432], P(None, 'q')
- output 2: float32 [25], replicated
All inputs are finite; a program needn't handle non-finite values.
Results may differ from a plain program's by a relative error of at most 0.001.
Values sent between devices are 32-bit elements.
A program may use at most 1 GiB of HBM per device.

v0:
```python
import jax
import jax.numpy as jnp
from jax import lax
from jax.sharding import PartitionSpec as P

LOW_BITS = 7
LANES = 2 ** LOW_BITS


def mix_pair(first, second, coef_a, coef_b):
    out_re = coef_a[0] * first[0] - coef_a[1] * first[1] + coef_b[0] * second[0] - coef_b[1] * second[1]
    out_im = coef_a[0] * first[1] + coef_a[1] * first[0] + coef_b[0] * second[1] + coef_b[1] * second[0]
    return jnp.stack([out_re, out_im])


def gate_wide(state, bit_pos, gate_mat):
    stride = state.shape[1] >> (bit_pos + 1)
    if stride >= 8 * LANES:
        view = state.reshape(2, 2 ** bit_pos, 2, stride // LANES, LANES)
        zero_half = view[:, :, 0]
        one_half = view[:, :, 1]
        new_zero = mix_pair(zero_half, one_half, gate_mat[:, 0, 0], gate_mat[:, 0, 1])
        new_one = mix_pair(zero_half, one_half, gate_mat[:, 1, 0], gate_mat[:, 1, 1])
        return jnp.stack([new_zero, new_one], axis=2).reshape(state.shape)
    view = state.reshape(2, 2 ** bit_pos, 2 * stride)
    zero_half = view[:, :, :stride]
    one_half = view[:, :, stride:]
    new_zero = mix_pair(zero_half, one_half, gate_mat[:, 0, 0], gate_mat[:, 0, 1])
    new_one = mix_pair(zero_half, one_half, gate_mat[:, 1, 0], gate_mat[:, 1, 1])
    return jnp.concatenate([new_zero, new_one], axis=2).reshape(state.shape)


def low_block(state, low_gates):
    block_re = jnp.ones((1, 1), jnp.float32)
    block_im = jnp.zeros((1, 1), jnp.float32)
    for bit_pos in range(LOW_BITS):
        tr_re = low_gates[0, bit_pos].T
        tr_im = low_gates[1, bit_pos].T
        next_re = block_re[:, None, :, None] * tr_re[None, :, None, :] - block_im[:, None, :, None] * tr_im[None, :, None, :]
        next_im = block_re[:, None, :, None] * tr_im[None, :, None, :] + block_im[:, None, :, None] * tr_re[None, :, None, :]
        block_size = 2 * block_re.shape[0]
        block_re = next_re.reshape(block_size, block_size)
        block_im = next_im.reshape(block_size, block_size)
    rows = state.reshape(2, -1, LANES)
    highest = lax.Precision.HIGHEST
    out_re = jnp.dot(rows[0], block_re, precision=highest, preferred_element_type=jnp.float32) - jnp.dot(rows[1], block_im, precision=highest, preferred_element_type=jnp.float32)
    out_im = jnp.dot(rows[0], block_im, precision=highest, preferred_element_type=jnp.float32) + jnp.dot(rows[1], block_re, precision=highest, preferred_element_type=jnp.float32)
    return jnp.stack([out_re, out_im]).reshape(state.shape)


def sign_grid(first_index, row_count, cz_pairs, num_qubits):
    row_index = lax.iota(jnp.int32, row_count)[:, None]
    col_index = lax.iota(jnp.int32, LANES)[None, :]
    flat_index = first_index + row_index * LANES + col_index
    parity = jnp.zeros_like(flat_index)
    for pair_pos in range(cz_pairs.shape[0]):
        shift_a = num_qubits - 1 - cz_pairs[pair_pos, 0]
        shift_b = num_qubits - 1 - cz_pairs[pair_pos, 1]
        parity = parity ^ ((flat_index >> shift_a) & (flat_index >> shift_b) & 1)
    return (1 - 2 * parity).astype(jnp.float32)


def bit_balance(density, row_bits):
    row_tot = jnp.sum(density, axis=1)
    col_tot = jnp.sum(density, axis=0)
    row_index = lax.iota(jnp.int32, density.shape[0])
    col_index = lax.iota(jnp.int32, LANES)
    row_part = [jnp.sum(row_tot * (1 - 2 * ((row_index >> (row_bits - 1 - bit_pos)) & 1)).astype(jnp.float32)) for bit_pos in range(row_bits)]
    col_part = [jnp.sum(col_tot * (1 - 2 * ((col_index >> (LOW_BITS - 1 - bit_pos)) & 1)).astype(jnp.float32)) for bit_pos in range(LOW_BITS)]
    return row_part + col_part


def solution(mesh):
    group_size = mesh.shape['q']
    top_bits = group_size.bit_length() - 1

    def local_layer(state_local, unitaries, cz_pairs):
        num_qubits = unitaries.shape[1]
        local_size = state_local.shape[1]
        row_count = local_size // LANES
        device = lax.axis_index('q')
        grid = state_local.reshape(2, row_count, LANES)
        for qubit_pos in range(top_bits):
            bit_shift = top_bits - 1 - qubit_pos
            flip_mask = 1 << bit_shift
            partner = lax.ppermute(grid, 'q', [(source, source ^ flip_mask) for source in range(group_size)])
            own_bit = (device >> bit_shift) & 1
            gate_mat = unitaries[:, qubit_pos]
            coef_self = jnp.where(own_bit == 1, gate_mat[:, 1, 1], gate_mat[:, 0, 0])
            coef_other = jnp.where(own_bit == 1, gate_mat[:, 1, 0], gate_mat[:, 0, 1])
            grid = mix_pair(grid, partner, coef_self, coef_other)
        state = grid.reshape(2, local_size)
        for qubit_pos in range(top_bits, num_qubits - LOW_BITS):
            state = gate_wide(state, qubit_pos - top_bits, unitaries[:, qubit_pos])
        state = low_block(state, unitaries[:, num_qubits - LOW_BITS:])
        grid = state.reshape(2, row_count, LANES) * sign_grid(device * local_size, row_count, cz_pairs, num_qubits)[None]
        density = grid[0] * grid[0] + grid[1] * grid[1]
        local_total = jnp.sum(density)
        top_part = [jnp.where(((device >> (top_bits - 1 - qubit_pos)) & 1) == 0, local_total, -local_total) for qubit_pos in range(top_bits)]
        low_part = bit_balance(density, num_qubits - top_bits - LOW_BITS)
        z_expect = lax.psum(jnp.stack(top_part + low_part), 'q') / (local_size * group_size)
        return grid.reshape(2, local_size), z_expect

    return jax.shard_map(local_layer, mesh=mesh, in_specs=(P(None, 'q'), P(), P()), out_specs=(P(None, 'q'), P()), check_vma=False)
```

profile of v0, /device:TPU:0, one launch (start us, length us, event | category | flops | bytes accessed | tf_op | source)
XLA Modules:
  0.0 1946.6 jit_solution(6039578454886926737)
XLA Ops:
  0.6 12.8 copy.307
  17.7 23.0 %multiply_add_fusion.4 = (f32[1,2097152]{1,0:T(1,128)}, f32[1,2097152]{1,0:T(1,128)}) fusion(f32[2,2097152]{1,0:T(2,128)} %param.3, f32[]{:T(128)} %bitcast.18, f32[]{:T(128)} %bitcast.17), kind=kLoop, calls=%fused_computation.55 | loop fusion | flops 12582912 | bytes 33554440 | tf_op jit(solution)/shard_map/add | solution.py:12
  41.2 335.8 %collective-permute-done = f32[2,16384,128]{2,1,0:T(8,128)} collective-permute-done((f32[2,16384,128]{2,1,0:T(8,128)}, f32[2,16384,128]{2,1,0:T(8,128)}, u32[]{:S(2)}, u32[]{:S(2)}) %collective-permute-start) | collective-permute-done | bytes 16777248 | tf_op jit(solution)/shard_map/ppermute | solution.py:86
  377.0 19.2 multiply_add_fusion.3
  396.2 6.5 pad_maximum_fusion
  405.5 358.7 %collective-permute-done.1 = f32[2,16384,128]{2,1,0:T(8,128)} collective-permute-done((f32[2,16384,128]{2,1,0:T(8,128)S(1)}, f32[2,16384,128]{2,1,0:T(8,128)}, u32[]{:S(2)}, u32[]{:S(2)}) %collective-permute-start.1) | collective-permute-done | bytes 16777248 | tf_op jit(solution)/shard_map/ppermute | solution.py:86
  764.2 21.1 %multiply_subtract_fusion.2 = (f32[1,16384,128]{2,1,0:T(8,128)}, f32[1,16384,128]{2,1,0:T(8,128)}) fusion(f32[1,16384,128]{2,1,0:T(8,128)} %get-tuple-element.104, f32[1,16384,128]{2,1,0:T(8,128)} %get-tuple-element.105, f32[2,16384,128]{2,1,0:T(8,128)} %collective-permute-done.1, f32[]{:T(128)} %bitcast.25, f32[]{:T(128)} %bitcast.24, f32[]{:T(128)} %bitcast.22, ...), kind=kLoop, calls=%fused_computation.53 | loop fusion | flops 29360128 | bytes 50331664 | tf_op jit(solution)/shard_map/sub | solution.py:11
  785.3 11.5 pad_maximum_fusion.1
  799.4 358.2 %collective-permute-done.2 = f32[2,16384,128]{2,1,0:T(8,128)} collective-permute-done((f32[2,16384,128]{2,1,0:T(8,128)}, f32[2,16384,128]{2,1,0:T(8,128)}, u32[]{:S(2)}, u32[]{:S(2)}) %collective-permute-start.2) | collective-permute-done | bytes 16777248 | tf_op jit(solution)/shard_map/ppermute | solution.py:86
  1157.5 21.2 %multiply_add_fusion.1 = (f32[1,16384,128]{2,1,0:T(8,128)}, f32[1,16384,128]{2,1,0:T(8,128)}) fusion(f32[1,16384,128]{2,1,0:T(8,128)} %get-tuple-element.62, f32[1,16384,128]{2,1,0:T(8,128)} %get-tuple-element.63, f32[2,16384,128]{2,1,0:T(8,128)} %collective-permute-done.2, f32[]{:T(128)} %bitcast.28, f32[]{:T(128)} %bitcast.27, f32[]{:T(128)} %bitcast.26, ...), kind=kLoop, calls=%fused_computation.50 | loop fusion | flops 29360128 | bytes 50331664 | tf_op jit(solution)/shard_map/add | solution.py:12
  1178.7 11.5 pad_maximum_fusion.2
  1229.7 19.4 subtract_convert_fusion
  1249.1 21.3 %multiply_subtract_fusion = (f32[1,16384,128]{2,1,0:T(8,128)}, f32[1,16384,128]{2,1,0:T(8,128)}) fusion(f32[1,16384,128]{2,1,0:T(8,128)} %get-tuple-element.60, f32[1,16384,128]{2,1,0:T(8,128)} %get-tuple-element.61, f32[2,16384,128]{2,1,0:T(8,128)} %collective-permute-done.3, f32[]{:T(128)} %bitcast.31, f32[]{:T(128)} %bitcast.30, f32[]{:T(128)} %bitcast.29, ...), kind=kLoop, calls=%fused_computation.49 | loop fusion | flops 29360128 | bytes 50331664 | tf_op jit(solution)/shard_map/sub | solution.py:11
  1270.5 16.1 multiply_subtract_fusion.13
  1286.6 9.4 multiply_add_fusion.13
  1301.7 5.8 subtract_bitcast_fusion.1
  1307.5 6.4 maximum_bitcast_fusion
  1313.8 6.2 subtract_bitcast_fusion
  1320.1 6.7 maximum_bitcast_fusion.1
  1347.9 6.2 pad_maximum_fusion.4
  1354.1 6.5 copy.183
  1377.0 6.2 pad_maximum_fusion.5
  1383.2 6.6 copy.193
  1406.8 6.2 pad_maximum_fusion.6
  1413.1 6.7 copy.203
  1437.4 6.2 pad_maximum_fusion.7
  1443.6 6.7 copy.213
  1454.7 5.8 fusion.37
  1469.1 6.2 pad_maximum_fusion.8
  1475.3 6.6 copy.223
  1486.6 5.8 fusion.28
  1502.3 6.2 pad_maximum_fusion.9
  1508.6 6.6 copy.233
  1519.8 6.0 fusion.19
  1534.8 6.4 pad_maximum_fusion.10
  1541.2 6.8 copy.243
  1564.8 6.2 pad_maximum_fusion.11
  1571.0 7.2 copy.253
  1596.3 6.3 copy.263
  1602.6 18.0 reshape_reshape.48
  1620.6 10.5 multiply_subtract_fusion.11
  1631.2 6.0 multiply_subtract_fusion.10
  1637.2 8.0 maximum_maximum_fusion.1
  1645.2 18.2 reshape_reshape.49
  1663.4 10.5 multiply_subtract_fusion.9
  1674.0 6.2 multiply_subtract_fusion.8
  1680.2 8.5 maximum_maximum_fusion.2
  1688.7 18.2 reshape_reshape.50
  1706.8 12.2 multiply_subtract_fusion.7
  1719.1 6.9 multiply_subtract_fusion.6
  1731.7 6.4 fusion.86
  1738.1 9.0 squeeze.470
  1747.1 9.0 squeeze.485
  1756.1 10.3 fusion.111
  1766.4 7.5 fusion.112
  1773.9 7.1 convolution_subtract_fusion
  1781.1 7.4 convolution_add_fusion
  1788.5 12.4 maximum_multiply_fusion.1
  1800.8 7.6 fusion.83
  1813.3 13.1 stack.445
  1826.3 47.3 %add.1539 = s32[16384,1,128]{2,1,0:T(1,128)S(1)} broadcast(s32[16384]{0:T(1024)S(1)} %copy-done.13), dimensions={0} | broadcast | bytes 8454144 | tf_op jit(solution)/shard_map/add | solution.py:54
  1873.6 18.2 subtract_convert_fusion.1
  1891.8 32.5 %psum.7 = f32[25]{0:T(128)S(1)} all-reduce(f32[25]{0:T(128)S(1)} %stack.445), channel_id=1, replica_groups=mesh['q'=16] {'q'}, use_global_device_ids=true, to_apply=%region_24.25 | all-reduce | flops 25 | bytes 200 | tf_op jit(solution)/shard_map/psum | solution.py:101
  1924.8 21.3 %maximum_multiply_fusion = f32[2,2097152]{1,0:T(2,128)} fusion(f32[1,2097152]{1,0:T(1,128)} %bitcast.967, f32[1,2097152]{1,0:T(1,128)} %bitcast.965, f32[2097152]{0:T(1024)} %subtract_convert_fusion.1), kind=kLoop, calls=%fused_computation.20 | loop fusion | flops 8388608 | bytes 41943040 | tf_op jit(solution)/shard_map/mul | solution.py:96
  (144 shorter events, 196.6 us)
Async XLA Ops:
  0.6 16.2 copy-start.9
  13.5 363.5 %collective-permute-start = (f32[2,16384,128]{2,1,0:T(8,128)}, f32[2,16384,128]{2,1,0:T(8,128)}, u32[]{:S(2)}, u32[]{:S(2)}) collective-permute-start(f32[2,16384,128]{2,1,0:T(8,128)} %bitcast.934), channel_id=1, source_target_pairs={{0,8},{1,9},{2,10},{3,11},{4,12},{5,13},{6,14},{7,15},{8,0},{9,1},... | collective-permute-start | bytes 50331656 | tf_op jit(solution)/shard_map/ppermute | solution.py:86
  402.7 361.5 %collective-permute-start.1 = (f32[2,16384,128]{2,1,0:T(8,128)S(1)}, f32[2,16384,128]{2,1,0:T(8,128)}, u32[]{:S(2)}, u32[]{:S(2)}) collective-permute-start(f32[2,16384,128]{2,1,0:T(8,128)S(1)} %pad_maximum_fusion), channel_id=1, source_target_pairs={{0,4},{1,5},{2,6},{3,7},{4,0},{5,1},{6,2},{7,3},{8,12},{9,13},{10,... | collective-permute-start | bytes 50331656 | tf_op jit(solution)/shard_map/ppermute | solution.py:86
  796.8 360.7 %collective-permute-start.2 = (f32[2,16384,128]{2,1,0:T(8,128)}, f32[2,16384,128]{2,1,0:T(8,128)}, u32[]{:S(2)}, u32[]{:S(2)}) collective-permute-start(f32[2,16384,128]{2,1,0:T(8,128)} %pad_maximum_fusion.1), channel_id=1, source_target_pairs={{0,2},{1,3},{2,0},{3,1},{4,6},{5,7},{6,4},{7,5},{8,10},{9,11},{10,... | collective-permute-start | bytes 50331656 | tf_op jit(solution)/shard_map/ppermute | solution.py:86
  1190.2 58.9 %collective-permute-start.3 = (f32[2,16384,128]{2,1,0:T(8,128)}, f32[2,16384,128]{2,1,0:T(8,128)}, u32[]{:S(2)}, u32[]{:S(2)}) collective-permute-start(f32[2,16384,128]{2,1,0:T(8,128)} %pad_maximum_fusion.2), channel_id=1, source_target_pairs={{0,1},{1,0},{2,3},{3,2},{4,5},{5,4},{6,7},{7,6},{8,9},{9,8},{10,11... | collective-permute-start | bytes 50331656 | tf_op jit(solution)/shard_map/ppermute | solution.py:86
  1198.8 9.1 copy-start.14
  1229.7 19.4 copy-start.12
  1270.4 16.1 copy-start.6
  1270.5 16.1 copy-start.7
  1320.1 6.7 copy-start.8
  1620.6 10.6 copy-start
  1663.4 10.6 copy-start.2
  1706.8 12.2 copy-start.1
  1747.1 9.0 copy-start.10
  1756.1 10.3 copy-start.5
  1756.1 10.3 copy-start.11
  1756.1 17.8 slice-start
  1766.4 7.5 slice-start.1
  1781.1 7.4 copy-start.3
  1788.4 12.4 copy-start.4
  1800.8 25.5 %copy-start.13 = (s32[16384]{0:T(1024)S(1)}, s32[16384]{0:T(1024)}, u32[]{:S(2)}) copy-start(s32[16384]{0:T(1024)} %copy-done.12) | copy-start | bytes 196612
where the time goes:
time: 1960 us; the launch traced here: 1950 us
  waiting for transfers between devices  1050 us (54%)
  other arithmetic  568 us (29%)
  local copies, waits for them, and re-layouts  236 us (12%)
  blocking collectives  32.5 us (2%)
  matrix products  32.3 us (2%)
    ppermute x4, waiting for transfers between devices, local_layer(): lax.ppermute(grid, 'q', [(source, source ^ flip_mask) for source in range...  1050 us
    sub x29, other arithmetic, mix_pair(): coef_a[0] * first[0] - coef_a[1] * first[1] + coef_b[0] * second[0]  199 us
    add x13, other arithmetic, mix_pair(): coef_a[0] * first[1] + coef_a[1] * first[0] + coef_b[0] * second[1]  121 us
    another operation x31, other arithmetic, gate_wide(): return jnp.stack([new_zero, new_one], axis=2).reshape(state.shape)  110 us
    another operation x9, local copies, waits for them, and re-layouts, gate_wide(): return jnp.stack([new_zero, new_one], axis=2).reshape(state.shape)  60 us
    another operation x3, local copies, waits for them, and re-layouts, gate_wide(): view = state.reshape(2, 2 ** bit_pos, 2 * stride)  54.3 us
    add x1, local copies, waits for them, and re-layouts, sign_grid(): flat_index = first_index + row_index * LANES + col_index  47.3 us
  transfers between devices with their start and end apart: 4, of which 3 were waited for; matrix products, arithmetic and copies ran while one was open for 4% of the time, Pallas kernels for 0%

commit v1 on v0

v1 whole, which is shorter than its diff:
```python
import functools
import jax
import jax.numpy as jnp
from jax import lax
from jax.experimental import pallas as pl
from jax.experimental.pallas import tpu as pltpu
from jax.sharding import PartitionSpec as P

MESH = pl.DeviceIdType.MESH
LANES = 128
LANE_BITS = 7
ROW_BITS = 7
MID_BITS = 5
QUARTERS = 4
BLOCKS = 2 ** MID_BITS
BLOCK_ROWS = 2 * 2 ** ROW_BITS
HALF = BLOCK_ROWS // 2
STEPS = 16
STEP_BLOCKS = BLOCKS // STEPS
TOP_BITS = 4
CORE = 3
HI_BITS = 2 + MID_BITS
HIGHEST = lax.Precision.HIGHEST


def apply_coefs(coef_a, coef_b, first, second):
    out_re = coef_a[0] * first[0] - coef_a[1] * first[1] + coef_b[0] * second[0] - coef_b[1] * second[1]
    out_im = coef_a[0] * first[1] + coef_a[1] * first[0] + coef_b[0] * second[1] + coef_b[1] * second[0]
    return out_re, out_im


def gate_coefs(gates_ref, qubit):
    return [[(gates_ref[0, row, col, qubit], gates_ref[1, row, col, qubit]) for col in range(2)] for row in range(2)]


def butterfly(values, gates):
    size = len(values)
    for gate_pos, gate in enumerate(gates):
        stride = size >> (gate_pos + 1)
        values = list(values)
        for pos in range(size):
            if pos & stride:
                continue
            zero_half, one_half = values[pos], values[pos + stride]
            values[pos] = apply_coefs(gate[0][0], gate[0][1], zero_half, one_half)
            values[pos + stride] = apply_coefs(gate[1][0], gate[1][1], zero_half, one_half)
    return values


def load_rows(ref, row, rows):
    return ref[pl.ds(2 * row, rows, stride=2), :], ref[pl.ds(2 * row + 1, rows, stride=2), :]


def store_rows(ref, row, rows, value):
    ref[pl.ds(2 * row, rows, stride=2), :] = value[0]
    ref[pl.ds(2 * row + 1, rows, stride=2), :] = value[1]


def gate_blocks(refs, gates, rows):
    @pl.loop(0, HALF // rows)
    def _(group):
        row = pl.multiple_of(group * rows, rows)
        values = butterfly([load_rows(ref, row, rows) for ref in refs], gates)
        for ref, value in zip(refs, values):
            store_rows(ref, row, rows, value)


def build_matrix(mat_ref, gates_ref, first_qubit, num_bits, transposed):
    size = 2 ** num_bits
    out_index = lax.broadcasted_iota(jnp.int32, (size, size), 1 if transposed else 0)
    in_index = lax.broadcasted_iota(jnp.int32, (size, size), 0 if transposed else 1)
    prod_re = jnp.ones((size, size), jnp.float32)
    prod_im = jnp.zeros((size, size), jnp.float32)
    for bit_pos in range(num_bits):
        gate = gate_coefs(gates_ref, first_qubit + bit_pos)
        mask = 2 ** (num_bits - 1 - bit_pos)
        out_one = (out_index & mask) != 0
        in_one = (in_index & mask) != 0
        fac_re, fac_im = [jnp.where(out_one, jnp.where(in_one, gate[1][1][part], gate[1][0][part]), jnp.where(in_one, gate[0][1][part], gate[0][0][part])) for part in range(2)]
        prod_re, prod_im = prod_re * fac_re - prod_im * fac_im, prod_re * fac_im + prod_im * fac_re
    mat_ref[0:size, 0:size] = prod_re
    mat_ref[size:, size:] = prod_re
    mat_ref[0:size, size:] = prod_im if transposed else -prod_im
    mat_ref[size:, 0:size] = -prod_im if transposed else prod_im


def kernel(group_size, x_ref, gates_ref, pairs_ref, out_ref, z_ref, recv_ref, lane_mat, row_mat, low_sum, high_sum, part_ref, parts_ref,
           mask_ref, load_sem, send_sem, recv_sem, part_send, part_recv):
    num_qubits = gates_ref.shape[3]
    num_pairs = pairs_ref.shape[1]
    me = lax.axis_index('q')
    strides = [group_size >> (link + 1) for link in range(TOP_BITS)]
    own_bits = [(me // stride) % 2 for stride in strides]
    partners = [me + stride * (1 - 2 * own_bit) for stride, own_bit in zip(strides, own_bits)]

    def blocks_of(quarter, step):
        return out_ref.at[quarter, pl.ds(step * STEP_BLOCKS, STEP_BLOCKS)]

    def load(step):
        span = pl.ds(step * STEP_BLOCKS, STEP_BLOCKS)
        return pltpu.make_async_copy(x_ref.at[:, span], out_ref.at[:, span], load_sem.at[step])

    def exchange(link, slot, step):
        return pltpu.make_async_remote_copy(
            src_ref=blocks_of((slot + link) % 4, step), dst_ref=recv_ref.at[link, slot % 2, pl.ds(step * STEP_BLOCKS, STEP_BLOCKS)],
            send_sem=send_sem.at[link, step], recv_sem=recv_sem.at[link, slot % 2, step],
            device_id=(partners[link],), device_id_type=MESH)

    def send_links(slot, step):
        for link in range(CORE):
            exchange(link, slot, step).start()

    @pl.loop(0, STEPS)
    def _(step):
        load(step).start()

    barrier = pltpu.get_barrier_semaphore()
    for offset in range(1, group_size):
        pl.semaphore_signal(barrier, inc=1, device_id=((me + offset) % group_size,), device_id_type=MESH)

    for pair_pos in range(num_pairs):
        mask_ref[pair_pos] = (1 << (num_qubits - 1 - pairs_ref[0, pair_pos])) | (1 << (num_qubits - 1 - pairs_ref[1, pair_pos]))
    low_sum[...] = jnp.zeros_like(low_sum)
    high_sum[...] = jnp.zeros_like(high_sum)
    pl.semaphore_wait(barrier, group_size - 1)

    quarter_gates = [gate_coefs(gates_ref, TOP_BITS), gate_coefs(gates_ref, TOP_BITS + 1)]

    @pl.loop(0, STEPS)
    def _(step):
        @pl.when(step > 0)
        def _():
            send_links(0, step - 1)

        load(step).wait()
        for block in range(STEP_BLOCKS):
            gate_blocks([out_ref.at[quarter, step * STEP_BLOCKS + block] for quarter in range(QUARTERS)], quarter_gates, 16)

    def mid_gates(quarter):
        first = TOP_BITS + 2
        gates = [gate_coefs(gates_ref, first + bit_pos) for bit_pos in range(MID_BITS)]

        @pl.loop(0, BLOCKS // 8)
        def _(low):
            gate_blocks([out_ref.at[quarter, pos * (BLOCKS // 8) + low] for pos in range(8)], gates[:3], 8)

        @pl.loop(0, BLOCKS // 4)
        def _(high):
            gate_blocks([out_ref.at[quarter, high * 4 + pos] for pos in range(4)], gates[3:], 16)

    def finish(quarter, block, row, rows, value):
        first_row = ((me * QUARTERS + quarter) * BLOCKS + block) * HALF + row
        index = first_row * LANES + lax.broadcasted_iota(jnp.int32, (rows, LANES), 0) * LANES + lax.broadcasted_iota(jnp.int32, (rows, LANES), 1)
        odd = None
        for pair_pos in range(num_pairs):
            mask = mask_ref[pair_pos]
            hit = (index & mask) == mask
            odd = hit if odd is None else jnp.logical_xor(odd, hit)
        sign = jnp.where(odd, -1.0, 1.0)
        value = (value[0] * sign, value[1] * sign)
        store_rows(out_ref.at[quarter, block], row, rows, value)
        density = value[0] * value[0] + value[1] * value[1]
        low_sum[pl.ds(row, rows), :] += density
        return jnp.sum(density.reshape(rows // 8, 8, LANES), axis=0)

    def add_high(quarter, block, total):
        position = quarter * BLOCKS + block
        for bit_pos in range(HI_BITS):
            bit = (position // 2 ** (HI_BITS - 1 - bit_pos)) % 2
            high_sum[bit_pos] += total * (1 - 2 * bit).astype(jnp.float32)
        high_sum[HI_BITS] += total

    def mix(link, slot, step, last):
        quarter = (slot + link) % 4
        own_bit = own_bits[link]
        coef_self = [gates_ref[part, own_bit, own_bit, link] for part in range(2)]
        coef_other = [gates_ref[part, own_bit, 1 - own_bit, link] for part in range(2)]
        rows = 32
        for step_block in range(STEP_BLOCKS):
            block = step * STEP_BLOCKS + step_block
            own_ref = out_ref.at[quarter, block]
            other_ref = recv_ref.at[link, slot % 2, block]

            def body(group, total):
                row = pl.multiple_of(group * rows, rows)
                value = apply_coefs(coef_self, coef_other, load_rows(own_ref, row, rows), load_rows(other_ref, row, rows))
                if last:
                    return total + finish(quarter, block, row, rows, value)
                store_rows(own_ref, row, rows, value)
                return total

            total = lax.fori_loop(0, HALF // rows, body, jnp.zeros((8, LANES), jnp.float32))
            if last:
                add_high(quarter, block, total)

    def local(slot, step, last):
        quarter = (slot + CORE) % 4
        copy = exchange(CORE, slot, step)
        copy.wait_recv()
        copy.wait_send()
        mix(CORE, slot, step, False)
        refs = [out_ref.at[quarter, step * STEP_BLOCKS + block] for block in range(STEP_BLOCKS)]
        parts = [load_rows(ref, 0, HALF) for ref in refs]
        rows = jnp.concatenate([jnp.concatenate(part, axis=1) for part in parts], axis=0)
        mixed = jnp.dot(rows, lane_mat[...], precision=HIGHEST, preferred_element_type=jnp.float32)
        columns = jnp.concatenate([
            jnp.concatenate([mixed[block * HALF:(block + 1) * HALF, :LANES], mixed[block * HALF:(block + 1) * HALF, LANES:]], axis=0)
            for block in range(STEP_BLOCKS)], axis=1)
        done = jnp.dot(row_mat[...], columns, precision=HIGHEST, preferred_element_type=jnp.float32)
        for block, ref in enumerate(refs):
            piece = done[:, block * LANES:(block + 1) * LANES]
            store_rows(ref, 0, HALF, (piece[:HALF], piece[HALF:]))
        if last:
            rows_now = 32
            for step_block in range(STEP_BLOCKS):
                block = step * STEP_BLOCKS + step_block

                def body(group, total):
                    row = pl.multiple_of(group * rows_now, rows_now)
                    return total + finish(quarter, block, row, rows_now, load_rows(out_ref.at[quarter, block], row, rows_now))

                total = lax.fori_loop(0, HALF // rows_now, body, jnp.zeros((8, LANES), jnp.float32))
                add_high(quarter, block, total)

    for slot in range(QUARTERS):
        mid_gates((slot + CORE) % 4)
        send_links(slot, STEPS - 1)

        @pl.loop(0, STEPS)
        def _(step):
            exchange(CORE, slot, step).start()

        if slot == 0:
            build_matrix(lane_mat, gates_ref, num_qubits - LANE_BITS, LANE_BITS, True)
            build_matrix(row_mat, gates_ref, num_qubits - LANE_BITS - ROW_BITS, ROW_BITS, False)
        last = slot == QUARTERS - 1

        @pl.loop(0, STEPS)
        def _(step):
            if not last:
                @pl.when(step > 0)
                def _():
                    send_links(slot + 1, step - 1)
            local(slot, step, last)
            for link in range(CORE):
                copy = exchange(link, slot, step)
                copy.wait_recv()
                copy.wait_send()
                mix(link, slot, step, last)

    total = high_sum[HI_BITS]
    sublane = lax.broadcasted_iota(jnp.int32, (8, LANES), 0)
    lane = lax.broadcasted_iota(jnp.int32, (8, LANES), 1)
    signed = [total * (1 - 2 * own_bit).astype(jnp.float32) for own_bit in own_bits]
    signed += [high_sum[bit_pos] for bit_pos in range(HI_BITS)]
    low = [low_sum[8 * pos:8 * pos + 8, :] for pos in range(HALF // 8)]
    for bit_pos in range(ROW_BITS - 3):
        mask = 2 ** (ROW_BITS - 4 - bit_pos)
        signed.append(functools.reduce(jnp.add, [-part if pos & mask else part for pos, part in enumerate(low)]))
    signed += [jnp.where((sublane & (4 >> bit_pos)) != 0, -total, total) for bit_pos in range(3)]
    signed += [jnp.where((lane & (64 >> bit_pos)) != 0, -total, total) for bit_pos in range(LANE_BITS)]
    rows = [jnp.sum(part, axis=0, keepdims=True) for part in signed]
    table = jnp.concatenate(rows + [jnp.zeros((LANES - len(rows), LANES), jnp.float32)], axis=0)
    part = lax.dot_general(jnp.ones((8, LANES), jnp.float32), table, (((1,), (1,)), ((), ())), precision=HIGHEST, preferred_element_type=jnp.float32)
    part_ref[...] = part

    def share(offset):
        return pltpu.make_async_remote_copy(
            src_ref=part_ref, dst_ref=parts_ref.at[me], send_sem=part_send.at[offset], recv_sem=part_recv.at[me],
            device_id=((me + offset) % group_size,), device_id_type=MESH)

    def shared(offset):
        source = (me + group_size - offset) % group_size
        return pltpu.make_async_remote_copy(
            src_ref=part_ref, dst_ref=parts_ref.at[source], send_sem=part_send.at[offset], recv_sem=part_recv.at[source],
            device_id=((me + offset) % group_size,), device_id_type=MESH)

    for offset in range(1, group_size):
        share(offset).start()
    parts_ref[me] = part
    for offset in range(1, group_size):
        shared(offset).wait_recv()
    for offset in range(1, group_size):
        share(offset).wait_send()
    z_ref[...] = functools.reduce(jnp.add, [parts_ref[pos] for pos in range(group_size)]) * (1.0 / 2 ** num_qubits)


def solution(mesh):
    group_size = mesh.shape['q']

    def local_layer(state_local, unitaries, cz_pairs):
        num_qubits = unitaries.shape[1]
        local_size = state_local.shape[1]
        row_count = local_size // LANES
        shape = (QUARTERS, BLOCKS, BLOCK_ROWS, LANES)
        grid = state_local.reshape(2, row_count, LANES).transpose(1, 0, 2).reshape(shape)
        state, sums = pl.pallas_call(
            functools.partial(kernel, group_size),
            out_shape=(pltpu.VMEM(shape, jnp.float32), jax.ShapeDtypeStruct((8, LANES), jnp.float32)),
            in_specs=[pl.BlockSpec(memory_space=pl.ANY), pl.BlockSpec(memory_space=pltpu.SMEM), pl.BlockSpec(memory_space=pltpu.SMEM)],
            out_specs=(pl.BlockSpec(memory_space=pltpu.VMEM), pl.BlockSpec(memory_space=pltpu.VMEM)),
            scratch_shapes=[
                pltpu.VMEM((TOP_BITS, 2, BLOCKS, BLOCK_ROWS, LANES), jnp.float32),
                pltpu.VMEM((2 * LANES, 2 * LANES), jnp.float32),
                pltpu.VMEM((BLOCK_ROWS, BLOCK_ROWS), jnp.float32),
                pltpu.VMEM((HALF, LANES), jnp.float32),
                pltpu.VMEM((HI_BITS + 1, 8, LANES), jnp.float32),
                pltpu.VMEM((8, LANES), jnp.float32),
                pltpu.VMEM((group_size, 8, LANES), jnp.float32),
                pltpu.SMEM((cz_pairs.shape[0],), jnp.int32),
                pltpu.SemaphoreType.DMA((STEPS,)),
                pltpu.SemaphoreType.DMA((TOP_BITS, STEPS)),
                pltpu.SemaphoreType.DMA((TOP_BITS, 2, STEPS)),
                pltpu.SemaphoreType.DMA((group_size,)),
                pltpu.SemaphoreType.DMA((group_size,)),
            ],
            compiler_params=pltpu.CompilerParams(collective_id=0, has_side_effects=True, vmem_limit_bytes=44 * 1024 * 1024),
        )(grid, unitaries.transpose(0, 2, 3, 1), cz_pairs.T)
        state = state.reshape(row_count, 2, LANES).transpose(1, 0, 2).reshape(2, local_size)
        return state, sums[0, :num_qubits]

    return jax.shard_map(local_layer, mesh=mesh, in_specs=(P(None, 'q'), P(), P()), out_specs=(P(None, 'q'), P()), check_vma=False)
```

time: 1960 us -> 383 us (0.20)
  waiting for transfers between devices: 1050 us -> 0 us
  other arithmetic: 568 us -> 0 us
  Pallas kernels: 0 us -> 375 us
  local copies, waits for them, and re-layouts: 236 us -> 7.34 us
  blocking collectives: 32.5 us -> 0 us
  matrix products: 32.3 us -> 0 us
    ppermute x4 -> x0, waiting for transfers between devices: 1050 us -> none  [local_layer(): lax.ppermute(grid, 'q', [(source, source ^ flip_mask) for source in range...]
    pallas_call x0 -> x1, Pallas kernels: none -> 375 us  [local_layer(): pl.pallas_call(functools.partial(kernel, group_size), out_shape=(pltpu.VM...]
    sub x36 -> x0, other arithmetic: 204 us -> none  [the longest x29 199 us: mix_pair(): coef_a[0] * first[0] - coef_a[1] * first[1] + coef_b[0] * second[0]]
    another operation x34 -> x0, other arithmetic: 140 us -> none  [the longest x31 110 us: gate_wide(): return jnp.stack([new_zero, new_one], axis=2).reshape(state.shape)]
    another operation x13 -> x0, local copies, waits for them, and re-layouts: 127 us -> none  [the longest x9 60 us: gate_wide(): return jnp.stack([new_zero, new_one], axis=2).reshape(state.shape)]
    add x14 -> x0, other arithmetic: 121 us -> none  [the longest x13 121 us: mix_pair(): coef_a[0] * first[1] + coef_a[1] * first[0] + coef_b[0] * second[1]]
    add x8 -> x0, local copies, waits for them, and re-layouts: 52.9 us -> none  [the longest x1 47.3 us: sign_grid(): flat_index = first_index + row_index * LANES + col_index]
    convert_element_type x2 -> x0, other arithmetic: 37.6 us -> none  [sign_grid(): return (1 - 2 * parity).astype(jnp.float32)]
  transfers between devices with their start and end apart: 4 -> 0, of which waited for: 3 -> 0; matrix products, arithmetic and copies ran while one was open for 4% -> 0% of each run, Pallas kernels for 0% -> 0%
where the time goes in v1:
time: 383 us
  Pallas kernels  375 us (98%)
  local copies, waits for them, and re-layouts  7.34 us (2%)
    pallas_call x1, Pallas kernels, local_layer(): pl.pallas_call(functools.partial(kernel, group_size), out_shape=(pltpu.VM...  375 us

profile of v1, /device:TPU:0, one launch (start us, length us, event | category | flops | bytes accessed | tf_op | source)
XLA Modules:
  0.0 383.1 jit_solution(6159869640658841189)
XLA Ops:
  0.6 375.1 %shard_map.50 = (f32[4,32,256,128]{3,2,1,0:T(8,128)S(1)}, f32[8,128]{1,0:T(8,128)}) custom-call(f32[4,32,256,128]{3,2,1,0:T(8,128)} %bitcast.15, f32[2,2,2,25]{3,2,1,0:T(2,128)} %bitcast.16, s32[2,12]{1,0:T(2,128)} %bitcast.17), custom_call_target="tpu_custom_call" | custom-call | tf_op jit(solution)/shard_map/pallas_call | solution.py:297
  375.8 6.2 %copy.8 = f32[2,2097152]{1,0:T(2,128)} copy(f32[2,2097152]{1,0:T(2,128)S(1)} %bitcast.14) | data formatting | bytes 33554432
  381.9 1.2 slice_bitcast_fusion

commit v2 on v1

--- a/solution.py
+++ b/solution.py
@@ -15,8 +15,12 @@
 BLOCKS = 2 ** MID_BITS
 BLOCK_ROWS = 2 * 2 ** ROW_BITS
 HALF = BLOCK_ROWS // 2
-STEPS = 16
-STEP_BLOCKS = BLOCKS // STEPS
+LOCAL_BLOCKS = 2
+LOAD_SPANS = (1, 6, 9, 16)
+LINK_SPANS = ((1, 6, 9, 16), (16, 16), (16, 16), (16, 11, 4, 1))
+CORE_SPANS = (8, 8, 8, 8)
+MAX_PIECES = 4
+FLUSH_PIECES = 1
 TOP_BITS = 4
 CORE = 3
 HI_BITS = 2 + MID_BITS
@@ -31,6 +35,11 @@
 
 def gate_coefs(gates_ref, qubit):
     return [[(gates_ref[0, row, col, qubit], gates_ref[1, row, col, qubit]) for col in range(2)] for row in range(2)]
+
+
+def pieces_of(spans):
+    starts = [sum(spans[:pos]) for pos in range(len(spans))]
+    return list(zip(starts, spans))
 
 
 def butterfly(values, gates):
@@ -84,57 +93,60 @@
     mat_ref[size:, 0:size] = -prod_im if transposed else prod_im
 
 
-def kernel(group_size, x_ref, gates_ref, pairs_ref, out_ref, z_ref, recv_ref, lane_mat, row_mat, low_sum, high_sum, part_ref, parts_ref,
-           mask_ref, load_sem, send_sem, recv_sem, part_send, part_recv):
-    num_qubits = gates_ref.shape[3]
-    num_pairs = pairs_ref.shape[1]
+def kernel(group_size, x_ref, gates_hbm, pairs_hbm, out_ref, parts_ref, recv_ref, lane_mat, row_mat, low_sum, high_sum, part_ref,
+           gates_ref, pairs_ref, mask_ref, small_sem, ready_sem, load_sem, send_sem, recv_sem, part_send, part_recv):
+    num_qubits = gates_hbm.shape[3]
+    num_pairs = pairs_hbm.shape[1]
     me = lax.axis_index('q')
     strides = [group_size >> (link + 1) for link in range(TOP_BITS)]
     own_bits = [(me // stride) % 2 for stride in strides]
     partners = [me + stride * (1 - 2 * own_bit) for stride, own_bit in zip(strides, own_bits)]
 
-    def blocks_of(quarter, step):
-        return out_ref.at[quarter, pl.ds(step * STEP_BLOCKS, STEP_BLOCKS)]
-
-    def load(step):
-        span = pl.ds(step * STEP_BLOCKS, STEP_BLOCKS)
-        return pltpu.make_async_copy(x_ref.at[:, span], out_ref.at[:, span], load_sem.at[step])
-
-    def exchange(link, slot, step):
+    load_pieces = pieces_of(LOAD_SPANS)
+    link_pieces = [pieces_of(spans) for spans in LINK_SPANS]
+    core_pieces = pieces_of(CORE_SPANS)
+
+    def load(piece):
+        span = pl.ds(*load_pieces[piece])
+        return pltpu.make_async_copy(x_ref.at[:, span], out_ref.at[:, span], load_sem.at[piece])
+
+    def exchange(link, slot, piece):
+        span = pl.ds(*(core_pieces if link == CORE else link_pieces[slot])[piece])
         return pltpu.make_async_remote_copy(
-            src_ref=blocks_of((slot + link) % 4, step), dst_ref=recv_ref.at[link, slot % 2, pl.ds(step * STEP_BLOCKS, STEP_BLOCKS)],
-            send_sem=send_sem.at[link, step], recv_sem=recv_sem.at[link, slot % 2, step],
+            src_ref=out_ref.at[(slot + link) % 4, span], dst_ref=recv_ref.at[link, slot % 2, span],
+            send_sem=send_sem.at[link, slot % 2, piece], recv_sem=recv_sem.at[link, slot % 2, piece],
             device_id=(partners[link],), device_id_type=MESH)
 
-    def send_links(slot, step):
-        for link in range(CORE):
-            exchange(link, slot, step).start()
-
-    @pl.loop(0, STEPS)
-    def _(step):
-        load(step).start()
+    def send_links(slot, done_from, done_to):
+        for piece, (start, size) in enumerate(link_pieces[slot]):
+            if done_from < start + size <= done_to:
+                for link in range(CORE):
+                    exchange(link, slot, piece).start()
 
     barrier = pltpu.get_barrier_semaphore()
-    for offset in range(1, group_size):
-        pl.semaphore_signal(barrier, inc=1, device_id=((me + offset) % group_size,), device_id_type=MESH)
-
-    for pair_pos in range(num_pairs):
-        mask_ref[pair_pos] = (1 << (num_qubits - 1 - pairs_ref[0, pair_pos])) | (1 << (num_qubits - 1 - pairs_ref[1, pair_pos]))
-    low_sum[...] = jnp.zeros_like(low_sum)
-    high_sum[...] = jnp.zeros_like(high_sum)
-    pl.semaphore_wait(barrier, group_size - 1)
+    for partner in partners:
+        pl.semaphore_signal(barrier, inc=1, device_id=(partner,), device_id_type=MESH)
+    small = [pltpu.make_async_copy(gates_hbm, gates_ref, small_sem.at[0]), pltpu.make_async_copy(pairs_hbm, pairs_ref, small_sem.at[1])]
+    load(0).start()
+    for copy in small:
+        copy.start()
+    for piece in range(1, len(load_pieces)):
+        load(piece).start()
+    for copy in small:
+        copy.wait()
 
     quarter_gates = [gate_coefs(gates_ref, TOP_BITS), gate_coefs(gates_ref, TOP_BITS + 1)]
 
-    @pl.loop(0, STEPS)
-    def _(step):
-        @pl.when(step > 0)
-        def _():
-            send_links(0, step - 1)
-
-        load(step).wait()
-        for block in range(STEP_BLOCKS):
-            gate_blocks([out_ref.at[quarter, step * STEP_BLOCKS + block] for quarter in range(QUARTERS)], quarter_gates, 16)
+    for piece, (start, size) in enumerate(load_pieces):
+        load(piece).wait()
+
+        @pl.loop(start, start + size)
+        def _(block):
+            gate_blocks([out_ref.at[quarter, block] for quarter in range(QUARTERS)], quarter_gates, 16)
+
+        if piece == 0:
+            pl.semaphore_wait(barrier, TOP_BITS)
+        send_links(0, start, start + size)
 
     def mid_gates(quarter):
         first = TOP_BITS + 2
@@ -170,83 +182,88 @@
             high_sum[bit_pos] += total * (1 - 2 * bit).astype(jnp.float32)
         high_sum[HI_BITS] += total
 
-    def mix(link, slot, step, last):
+    def mix(link, slot, block, last):
         quarter = (slot + link) % 4
         own_bit = own_bits[link]
         coef_self = [gates_ref[part, own_bit, own_bit, link] for part in range(2)]
         coef_other = [gates_ref[part, own_bit, 1 - own_bit, link] for part in range(2)]
         rows = 32
-        for step_block in range(STEP_BLOCKS):
-            block = step * STEP_BLOCKS + step_block
-            own_ref = out_ref.at[quarter, block]
-            other_ref = recv_ref.at[link, slot % 2, block]
-
-            def body(group, total):
-                row = pl.multiple_of(group * rows, rows)
-                value = apply_coefs(coef_self, coef_other, load_rows(own_ref, row, rows), load_rows(other_ref, row, rows))
-                if last:
-                    return total + finish(quarter, block, row, rows, value)
-                store_rows(own_ref, row, rows, value)
-                return total
-
-            total = lax.fori_loop(0, HALF // rows, body, jnp.zeros((8, LANES), jnp.float32))
+        own_ref = out_ref.at[quarter, block]
+        other_ref = recv_ref.at[link, slot % 2, block]
+
+        def body(group, total):
+            row = pl.multiple_of(group * rows, rows)
+            value = apply_coefs(coef_self, coef_other, load_rows(own_ref, row, rows), load_rows(other_ref, row, rows))
             if last:
-                add_high(quarter, block, total)
-
-    def local(slot, step, last):
+                return total + finish(quarter, block, row, rows, value)
+            store_rows(own_ref, row, rows, value)
+            return total
+
+        total = lax.fori_loop(0, HALF // rows, body, jnp.zeros((8, LANES), jnp.float32))
+        if last:
+            add_high(quarter, block, total)
+
+    def local(slot, first_block, last):
         quarter = (slot + CORE) % 4
-        copy = exchange(CORE, slot, step)
-        copy.wait_recv()
-        copy.wait_send()
-        mix(CORE, slot, step, False)
-        refs = [out_ref.at[quarter, step * STEP_BLOCKS + block] for block in range(STEP_BLOCKS)]
+        blocks = [first_block + pos for pos in range(LOCAL_BLOCKS)]
+        for block in blocks:
+            mix(CORE, slot, block, False)
+        refs = [out_ref.at[quarter, block] for block in blocks]
         parts = [load_rows(ref, 0, HALF) for ref in refs]
         rows = jnp.concatenate([jnp.concatenate(part, axis=1) for part in parts], axis=0)
         mixed = jnp.dot(rows, lane_mat[...], precision=HIGHEST, preferred_element_type=jnp.float32)
         columns = jnp.concatenate([
-            jnp.concatenate([mixed[block * HALF:(block + 1) * HALF, :LANES], mixed[block * HALF:(block + 1) * HALF, LANES:]], axis=0)
-            for block in range(STEP_BLOCKS)], axis=1)
+            jnp.concatenate([mixed[pos * HALF:(pos + 1) * HALF, :LANES], mixed[pos * HALF:(pos + 1) * HALF, LANES:]], axis=0)
+            for pos in range(LOCAL_BLOCKS)], axis=1)
         done = jnp.dot(row_mat[...], columns, precision=HIGHEST, preferred_element_type=jnp.float32)
-        for block, ref in enumerate(refs):
-            piece = done[:, block * LANES:(block + 1) * LANES]
+        for pos, ref in enumerate(refs):
+            piece = done[:, pos * LANES:(pos + 1) * LANES]
             store_rows(ref, 0, HALF, (piece[:HALF], piece[HALF:]))
         if last:
-            rows_now = 32
-            for step_block in range(STEP_BLOCKS):
-                block = step * STEP_BLOCKS + step_block
-
+            group_rows = 32
+            for block in blocks:
                 def body(group, total):
-                    row = pl.multiple_of(group * rows_now, rows_now)
-                    return total + finish(quarter, block, row, rows_now, load_rows(out_ref.at[quarter, block], row, rows_now))
-
-                total = lax.fori_loop(0, HALF // rows_now, body, jnp.zeros((8, LANES), jnp.float32))
+                    row = pl.multiple_of(group * group_rows, group_rows)
+                    return total + finish(quarter, block, row, group_rows, load_rows(out_ref.at[quarter, block], row, group_rows))
+
+                total = lax.fori_loop(0, HALF // group_rows, body, jnp.zeros((8, LANES), jnp.float32))
                 add_high(quarter, block, total)
 
+    for pair_pos in range(num_pairs):
+        mask_ref[pair_pos] = (1 << (num_qubits - 1 - pairs_ref[0, pair_pos])) | (1 << (num_qubits - 1 - pairs_ref[1, pair_pos]))
+    low_sum[...] = jnp.zeros_like(low_sum)
+    high_sum[...] = jnp.zeros_like(high_sum)
+    for link, partner in enumerate(partners):
+        pl.semaphore_signal(ready_sem.at[link], inc=1, device_id=(partner,), device_id_type=MESH)
+        pl.semaphore_wait(ready_sem.at[link], 1)
+    build_matrix(lane_mat, gates_ref, num_qubits - LANE_BITS, LANE_BITS, True)
+    build_matrix(row_mat, gates_ref, num_qubits - LANE_BITS - ROW_BITS, ROW_BITS, False)
     for slot in range(QUARTERS):
+        last = slot == QUARTERS - 1
         mid_gates((slot + CORE) % 4)
-        send_links(slot, STEPS - 1)
-
-        @pl.loop(0, STEPS)
-        def _(step):
-            exchange(CORE, slot, step).start()
-
-        if slot == 0:
-            build_matrix(lane_mat, gates_ref, num_qubits - LANE_BITS, LANE_BITS, True)
-            build_matrix(row_mat, gates_ref, num_qubits - LANE_BITS - ROW_BITS, ROW_BITS, False)
-        last = slot == QUARTERS - 1
-
-        @pl.loop(0, STEPS)
-        def _(step):
-            if not last:
-                @pl.when(step > 0)
-                def _():
-                    send_links(slot + 1, step - 1)
-            local(slot, step, last)
+        for piece in range(len(core_pieces)):
+            exchange(CORE, slot, piece).start()
+        for piece, (start, size) in enumerate(core_pieces):
+            copy = exchange(CORE, slot, piece)
+            copy.wait_recv()
+            copy.wait_send()
+
+            @pl.loop(start // LOCAL_BLOCKS, (start + size) // LOCAL_BLOCKS)
+            def _(step):
+                local(slot, step * LOCAL_BLOCKS, last)
+
+        for piece, (start, size) in enumerate(link_pieces[slot]):
             for link in range(CORE):
-                copy = exchange(link, slot, step)
+                copy = exchange(link, slot, piece)
                 copy.wait_recv()
                 copy.wait_send()
-                mix(link, slot, step, last)
+
+                @pl.loop(start, start + size)
+                def _(block):
+                    mix(link, slot, block, last)
+
+            if not last:
+                send_links(slot + 1, start, start + size)
 
     total = high_sum[HI_BITS]
     sublane = lax.broadcasted_iota(jnp.int32, (8, LANES), 0)
@@ -282,7 +299,23 @@
         shared(offset).wait_recv()
     for offset in range(1, group_size):
         share(offset).wait_send()
-    z_ref[...] = functools.reduce(jnp.add, [parts_ref[pos] for pos in range(group_size)]) * (1.0 / 2 ** num_qubits)
+
+
+def flush_kernel(scale, state_ref, parts_ref, out_ref, z_hbm, z_ref, sem, z_sem):
+    size = BLOCKS // FLUSH_PIECES
+    copies = []
+    for quarter in range(QUARTERS):
+        for piece in range(FLUSH_PIECES):
+            span = pl.ds(piece * size, size)
+            copies.append(pltpu.make_async_copy(state_ref.at[quarter, span], out_ref.at[quarter, span], sem.at[quarter, piece]))
+    for copy in copies:
+        copy.start()
+    total = functools.reduce(jnp.add, [parts_ref[pos] for pos in range(parts_ref.shape[0])])
+    z_ref[...] = total[0:1, :z_ref.shape[1]] * scale
+    copies.append(pltpu.make_async_copy(z_ref, z_hbm, z_sem))
+    copies[-1].start()
+    for copy in copies:
+        copy.wait()
 
 
 def solution(mesh):
@@ -294,10 +327,10 @@
         row_count = local_size // LANES
         shape = (QUARTERS, BLOCKS, BLOCK_ROWS, LANES)
         grid = state_local.reshape(2, row_count, LANES).transpose(1, 0, 2).reshape(shape)
-        state, sums = pl.pallas_call(
+        state, parts = pl.pallas_call(
             functools.partial(kernel, group_size),
-            out_shape=(pltpu.VMEM(shape, jnp.float32), jax.ShapeDtypeStruct((8, LANES), jnp.float32)),
-            in_specs=[pl.BlockSpec(memory_space=pl.ANY), pl.BlockSpec(memory_space=pltpu.SMEM), pl.BlockSpec(memory_space=pltpu.SMEM)],
+            out_shape=(pltpu.VMEM(shape, jnp.float32), pltpu.VMEM((group_size, 8, LANES), jnp.float32)),
+            in_specs=[pl.BlockSpec(memory_space=pl.ANY)] * 3,
             out_specs=(pl.BlockSpec(memory_space=pltpu.VMEM), pl.BlockSpec(memory_space=pltpu.VMEM)),
             scratch_shapes=[
                 pltpu.VMEM((TOP_BITS, 2, BLOCKS, BLOCK_ROWS, LANES), jnp.float32),
@@ -306,17 +339,28 @@
                 pltpu.VMEM((HALF, LANES), jnp.float32),
                 pltpu.VMEM((HI_BITS + 1, 8, LANES), jnp.float32),
                 pltpu.VMEM((8, LANES), jnp.float32),
-                pltpu.VMEM((group_size, 8, LANES), jnp.float32),
+                pltpu.SMEM((2, 2, 2, num_qubits), jnp.float32),
+                pltpu.SMEM((2, cz_pairs.shape[0]), jnp.int32),
                 pltpu.SMEM((cz_pairs.shape[0],), jnp.int32),
-                pltpu.SemaphoreType.DMA((STEPS,)),
-                pltpu.SemaphoreType.DMA((TOP_BITS, STEPS)),
-                pltpu.SemaphoreType.DMA((TOP_BITS, 2, STEPS)),
+                pltpu.SemaphoreType.DMA((2,)),
+                pltpu.SemaphoreType.REGULAR((TOP_BITS,)),
+                pltpu.SemaphoreType.DMA((len(LOAD_SPANS),)),
+                pltpu.SemaphoreType.DMA((TOP_BITS, 2, MAX_PIECES)),
+                pltpu.SemaphoreType.DMA((TOP_BITS, 2, MAX_PIECES)),
                 pltpu.SemaphoreType.DMA((group_size,)),
                 pltpu.SemaphoreType.DMA((group_size,)),
             ],
             compiler_params=pltpu.CompilerParams(collective_id=0, has_side_effects=True, vmem_limit_bytes=44 * 1024 * 1024),
         )(grid, unitaries.transpose(0, 2, 3, 1), cz_pairs.T)
+        state, z_expect = pl.pallas_call(
+            functools.partial(flush_kernel, 1.0 / 2 ** num_qubits),
+            out_shape=(jax.ShapeDtypeStruct(shape, jnp.float32), jax.ShapeDtypeStruct((1, num_qubits), jnp.float32)),
+            in_specs=[pl.BlockSpec(memory_space=pltpu.VMEM)] * 2,
+            out_specs=(pl.BlockSpec(memory_space=pl.ANY), pl.BlockSpec(memory_space=pl.ANY)),
+            scratch_shapes=[pltpu.VMEM((1, num_qubits), jnp.float32), pltpu.SemaphoreType.DMA((QUARTERS, FLUSH_PIECES)), pltpu.SemaphoreType.DMA],
+            compiler_params=pltpu.CompilerParams(vmem_limit_bytes=2 ** 20),
+        )(pltpu.with_memory_space_constraint(state, pltpu.VMEM), pltpu.with_memory_space_constraint(parts, pltpu.VMEM))
         state = state.reshape(row_count, 2, LANES).transpose(1, 0, 2).reshape(2, local_size)
-        return state, sums[0, :num_qubits]
+        return state, z_expect.reshape(num_qubits)
 
     return jax.shard_map(local_layer, mesh=mesh, in_specs=(P(None, 'q'), P(), P()), out_specs=(P(None, 'q'), P()), check_vma=False)

time: 383 us -> 378 us (0.987)
  local copies, waits for them, and re-layouts: 7.34 us -> 0 us
    unnamed x1 -> x0, local copies, waits for them, and re-layouts: 6.16 us -> none
    pallas_call x0 -> x1, Pallas kernels: none -> 5.96 us  [local_layer(): pl.pallas_call(functools.partial(flush_kernel, 1.0 / 2 ** num_qubits), ou...]
    pallas_call x1, Pallas kernels: 375 us -> 371 us  [local_layer(): pl.pallas_call(functools.partial(kernel, group_size), out_shape=(pltpu.VM...]
where the time goes in v2:
time: 378 us
  Pallas kernels  377 us (100%)
    pallas_call x1, Pallas kernels, local_layer(): pl.pallas_call(functools.partial(kernel, group_size), out_shape=(pltpu.VM...  371 us

profile of v2, /device:TPU:0, one launch (start us, length us, event | category | flops | bytes accessed | tf_op | source)
XLA Modules:
  0.0 377.5 jit_solution(13714178553840813318)
XLA Ops:
  0.6 370.8 %shard_map.50 = (f32[4,32,256,128]{3,2,1,0:T(8,128)S(1)}, f32[16,8,128]{2,1,0:T(8,128)S(1)}) custom-call(f32[4,32,256,128]{3,2,1,0:T(8,128)} %bitcast.13, f32[2,2,2,25]{3,2,1,0:T(2,128)} %bitcast.14, s32[2,12]{1,0:T(2,128)} %bitcast.15), custom_call_target="tpu_custom_call" | custom-call | tf_op jit(solution)/shard_map/pallas_call | solution.py:330
  371.4 6.0 %shard_map.51 = (f32[4,32,256,128]{3,2,1,0:T(8,128)}, f32[1,25]{1,0:T(1,128)}) custom-call(f32[4,32,256,128]{3,2,1,0:T(8,128)S(1)} %get-tuple-element.6.state_ref, f32[16,8,128]{2,1,0:T(8,128)S(1)} %get-tuple-element.7.parts_ref), custom_call_target="tpu_custom_call" | custom-call | tf_op jit(solution)/shard_map/pallas_call | solution.py:355

commit v3 on v2

--- a/solution.py
+++ b/solution.py
@@ -17,7 +17,8 @@
 HALF = BLOCK_ROWS // 2
 LOCAL_BLOCKS = 2
 LOAD_SPANS = (1, 6, 9, 16)
-LINK_SPANS = ((1, 6, 9, 16), (16, 16), (16, 16), (16, 11, 4, 1))
+LINK_SPANS = ((1, 6, 9, 16), (16, 16), (16, 16), (16, 10, 3))
+SWAP_BLOCKS = (29, 30, 31)
 CORE_SPANS = (8, 8, 8, 8)
 MAX_PIECES = 4
 FLUSH_PIECES = 1
@@ -93,8 +94,8 @@
     mat_ref[size:, 0:size] = -prod_im if transposed else prod_im
 
 
-def kernel(group_size, x_ref, gates_hbm, pairs_hbm, out_ref, parts_ref, recv_ref, lane_mat, row_mat, low_sum, high_sum, part_ref,
-           gates_ref, pairs_ref, mask_ref, small_sem, ready_sem, load_sem, send_sem, recv_sem, part_send, part_recv):
+def kernel(group_size, x_ref, gates_hbm, pairs_hbm, out_ref, parts_ref, recv_ref, lane_mat, row_mat, back_ref, low_sum, high_sum, sent_sum, part_ref,
+           gates_ref, pairs_ref, mask_ref, small_sem, ready_sem, swap_sem, load_sem, send_sem, recv_sem, part_send, part_recv):
     num_qubits = gates_hbm.shape[3]
     num_pairs = pairs_hbm.shape[1]
     me = lax.axis_index('q')
@@ -117,11 +118,30 @@
             send_sem=send_sem.at[link, slot % 2, piece], recv_sem=recv_sem.at[link, slot % 2, piece],
             device_id=(partners[link],), device_id_type=MESH)
 
+    def half_rows(bit):
+        return pl.ds(pl.multiple_of(bit * HALF, HALF), HALF)
+
+    def swap_out(link, swap):
+        quarter, block, rows = (QUARTERS - 1 + link) % 4, SWAP_BLOCKS[swap], half_rows(1 - own_bits[link])
+        return pltpu.make_async_remote_copy(
+            src_ref=out_ref.at[quarter, block, rows], dst_ref=recv_ref.at[link, 1, block, rows],
+            send_sem=swap_sem.at[0, link, swap], recv_sem=swap_sem.at[1, link, swap], device_id=(partners[link],), device_id_type=MESH)
+
+    def swap_back(link, swap):
+        return pltpu.make_async_remote_copy(
+            src_ref=recv_ref.at[link, 1, SWAP_BLOCKS[swap], half_rows(own_bits[link])], dst_ref=back_ref.at[link, swap],
+            send_sem=swap_sem.at[2, link, swap], recv_sem=swap_sem.at[3, link, swap], device_id=(partners[link],), device_id_type=MESH)
+
     def send_links(slot, done_from, done_to):
         for piece, (start, size) in enumerate(link_pieces[slot]):
             if done_from < start + size <= done_to:
                 for link in range(CORE):
                     exchange(link, slot, piece).start()
+        if slot == QUARTERS - 1:
+            for swap, block in enumerate(SWAP_BLOCKS):
+                if done_from <= block < done_to:
+                    for link in range(CORE):
+                        swap_out(link, swap).start()
 
     barrier = pltpu.get_barrier_semaphore()
     for partner in partners:
@@ -160,8 +180,8 @@
         def _(high):
             gate_blocks([out_ref.at[quarter, high * 4 + pos] for pos in range(4)], gates[3:], 16)
 
-    def finish(quarter, block, row, rows, value):
-        first_row = ((me * QUARTERS + quarter) * BLOCKS + block) * HALF + row
+    def finish(target_ref, device, quarter, block, row, rows, value):
+        first_row = ((device * QUARTERS + quarter) * BLOCKS + block) * HALF + row
         index = first_row * LANES + lax.broadcasted_iota(jnp.int32, (rows, LANES), 0) * LANES + lax.broadcasted_iota(jnp.int32, (rows, LANES), 1)
         odd = None
         for pair_pos in range(num_pairs):
@@ -170,7 +190,7 @@
             odd = hit if odd is None else jnp.logical_xor(odd, hit)
         sign = jnp.where(odd, -1.0, 1.0)
         value = (value[0] * sign, value[1] * sign)
-        store_rows(out_ref.at[quarter, block], row, rows, value)
+        store_rows(target_ref, row, rows, value)
         density = value[0] * value[0] + value[1] * value[1]
         low_sum[pl.ds(row, rows), :] += density
         return jnp.sum(density.reshape(rows // 8, 8, LANES), axis=0)
@@ -179,7 +199,7 @@
         position = quarter * BLOCKS + block
         for bit_pos in range(HI_BITS):
             bit = (position // 2 ** (HI_BITS - 1 - bit_pos)) % 2
-            high_sum[bit_pos] += total * (1 - 2 * bit).astype(jnp.float32)
+            high_sum[bit_pos] += total * jnp.asarray(1 - 2 * bit, jnp.float32)
         high_sum[HI_BITS] += total
 
     def mix(link, slot, block, last):
@@ -195,13 +215,33 @@
             row = pl.multiple_of(group * rows, rows)
             value = apply_coefs(coef_self, coef_other, load_rows(own_ref, row, rows), load_rows(other_ref, row, rows))
             if last:
-                return total + finish(quarter, block, row, rows, value)
+                return total + finish(own_ref, me, quarter, block, row, rows, value)
             store_rows(own_ref, row, rows, value)
             return total
 
         total = lax.fori_loop(0, HALF // rows, body, jnp.zeros((8, LANES), jnp.float32))
         if last:
             add_high(quarter, block, total)
+
+    def mix_swap(link, swap):
+        quarter, block = (QUARTERS - 1 + link) % 4, SWAP_BLOCKS[swap]
+        own_bit = own_bits[link]
+        home, away = [[[gates_ref[part, row_bit, col_bit, link] for part in range(2)] for col_bit in (own_bit, 1 - own_bit)] for row_bit in (own_bit, 1 - own_bit)]
+        rows = 32
+        own_ref = out_ref.at[quarter, block]
+        other_ref = recv_ref.at[link, 1, block]
+
+        def body(group, totals):
+            row = pl.multiple_of(own_bit * (HALF // 2) + group * rows, rows)
+            own, other = load_rows(own_ref, row, rows), load_rows(other_ref, row, rows)
+            kept = finish(own_ref, me, quarter, block, row, rows, apply_coefs(home[0], home[1], own, other))
+            sent = finish(other_ref, partners[link], quarter, block, row, rows, apply_coefs(away[0], away[1], own, other))
+            return totals[0] + kept, totals[1] + sent
+
+        zero = jnp.zeros((8, LANES), jnp.float32)
+        kept, sent = lax.fori_loop(0, HALF // 2 // rows, body, (zero, zero))
+        add_high(quarter, block, kept + sent)
+        sent_sum[link] += sent
 
     def local(slot, first_block, last):
         quarter = (slot + CORE) % 4
@@ -224,7 +264,7 @@
             for block in blocks:
                 def body(group, total):
                     row = pl.multiple_of(group * group_rows, group_rows)
-                    return total + finish(quarter, block, row, group_rows, load_rows(out_ref.at[quarter, block], row, group_rows))
+                    return total + finish(out_ref.at[quarter, block], me, quarter, block, row, group_rows, load_rows(out_ref.at[quarter, block], row, group_rows))
 
                 total = lax.fori_loop(0, HALF // group_rows, body, jnp.zeros((8, LANES), jnp.float32))
                 add_high(quarter, block, total)
@@ -233,6 +273,7 @@
         mask_ref[pair_pos] = (1 << (num_qubits - 1 - pairs_ref[0, pair_pos])) | (1 << (num_qubits - 1 - pairs_ref[1, pair_pos]))
     low_sum[...] = jnp.zeros_like(low_sum)
     high_sum[...] = jnp.zeros_like(high_sum)
+    sent_sum[...] = jnp.zeros_like(sent_sum)
     for link, partner in enumerate(partners):
         pl.semaphore_signal(ready_sem.at[link], inc=1, device_id=(partner,), device_id_type=MESH)
         pl.semaphore_wait(ready_sem.at[link], 1)
@@ -265,10 +306,20 @@
             if not last:
                 send_links(slot + 1, start, start + size)
 
+    for swap in range(len(SWAP_BLOCKS)):
+        for link in range(CORE):
+            copy = swap_out(link, swap)
+            copy.wait_recv()
+            copy.wait_send()
+            mix_swap(link, swap)
+        if swap < len(SWAP_BLOCKS) - 1:
+            for link in range(CORE):
+                swap_back(link, swap).start()
+
     total = high_sum[HI_BITS]
     sublane = lax.broadcasted_iota(jnp.int32, (8, LANES), 0)
     lane = lax.broadcasted_iota(jnp.int32, (8, LANES), 1)
-    signed = [total * (1 - 2 * own_bit).astype(jnp.float32) for own_bit in own_bits]
+    signed = [(total - 2.0 * sent_sum[link]) * (1 - 2 * own_bit).astype(jnp.float32) for link, own_bit in enumerate(own_bits)]
     signed += [high_sum[bit_pos] for bit_pos in range(HI_BITS)]
     low = [low_sum[8 * pos:8 * pos + 8, :] for pos in range(HALF // 8)]
     for bit_pos in range(ROW_BITS - 3):
@@ -294,7 +345,15 @@
 
     for offset in range(1, group_size):
         share(offset).start()
+    for link in range(CORE):
+        swap_back(link, len(SWAP_BLOCKS) - 1).start()
     parts_ref[me] = part
+    for swap in range(len(SWAP_BLOCKS)):
+        for link in range(CORE):
+            copy = swap_back(link, swap)
+            copy.wait_recv()
+            out_ref[(QUARTERS - 1 + link) % 4, SWAP_BLOCKS[swap], half_rows(1 - own_bits[link]), :] = back_ref[link, swap]
+            copy.wait_send()
     for offset in range(1, group_size):
         shared(offset).wait_recv()
     for offset in range(1, group_size):
@@ -336,14 +395,17 @@
                 pltpu.VMEM((TOP_BITS, 2, BLOCKS, BLOCK_ROWS, LANES), jnp.float32),
                 pltpu.VMEM((2 * LANES, 2 * LANES), jnp.float32),
                 pltpu.VMEM((BLOCK_ROWS, BLOCK_ROWS), jnp.float32),
+                pltpu.VMEM((CORE, len(SWAP_BLOCKS), HALF, LANES), jnp.float32),
                 pltpu.VMEM((HALF, LANES), jnp.float32),
                 pltpu.VMEM((HI_BITS + 1, 8, LANES), jnp.float32),
+                pltpu.VMEM((TOP_BITS, 8, LANES), jnp.float32),
                 pltpu.VMEM((8, LANES), jnp.float32),
                 pltpu.SMEM((2, 2, 2, num_qubits), jnp.float32),
                 pltpu.SMEM((2, cz_pairs.shape[0]), jnp.int32),
                 pltpu.SMEM((cz_pairs.shape[0],), jnp.int32),
                 pltpu.SemaphoreType.DMA((2,)),
                 pltpu.SemaphoreType.REGULAR((TOP_BITS,)),
+                pltpu.SemaphoreType.DMA((4, CORE, len(SWAP_BLOCKS))),
                 pltpu.SemaphoreType.DMA((len(LOAD_SPANS),)),
                 pltpu.SemaphoreType.DMA((TOP_BITS, 2, MAX_PIECES)),
                 pltpu.SemaphoreType.DMA((TOP_BITS, 2, MAX_PIECES)),

time: 378 us -> 374 us (0.989)
  Pallas kernels: 377 us -> 373 us
where the time goes in v3:
time: 374 us
  Pallas kernels  373 us (100%)
    pallas_call x1, Pallas kernels, local_layer(): pl.pallas_call(functools.partial(kernel, group_size), out_shape=(pltpu.VM...  367 us

profile of v3, /device:TPU:0, one launch (start us, length us, event | category | flops | bytes accessed | tf_op | source)
XLA Modules:
  0.0 374.2 jit_solution(4565262265972104401)
XLA Ops:
  0.6 367.4 %shard_map.50 = (f32[4,32,256,128]{3,2,1,0:T(8,128)S(1)}, f32[16,8,128]{2,1,0:T(8,128)S(1)}) custom-call(f32[4,32,256,128]{3,2,1,0:T(8,128)} %bitcast.13, f32[2,2,2,25]{3,2,1,0:T(2,128)} %bitcast.14, s32[2,12]{1,0:T(2,128)} %bitcast.15), custom_call_target="tpu_custom_call" | custom-call | tf_op jit(solution)/shard_map/pallas_call | solution.py:389
  368.1 6.0 %shard_map.51 = (f32[4,32,256,128]{3,2,1,0:T(8,128)}, f32[1,25]{1,0:T(1,128)}) custom-call(f32[4,32,256,128]{3,2,1,0:T(8,128)S(1)} %get-tuple-element.6.state_ref, f32[16,8,128]{2,1,0:T(8,128)S(1)} %get-tuple-element.7.parts_ref), custom_call_target="tpu_custom_call" | custom-call | tf_op jit(solution)/shard_map/pallas_call | solution.py:417

commit v4 on v3

--- a/solution.py
+++ b/solution.py
@@ -330,34 +330,38 @@
     rows = [jnp.sum(part, axis=0, keepdims=True) for part in signed]
     table = jnp.concatenate(rows + [jnp.zeros((LANES - len(rows), LANES), jnp.float32)], axis=0)
     part = lax.dot_general(jnp.ones((8, LANES), jnp.float32), table, (((1,), (1,)), ((), ())), precision=HIGHEST, preferred_element_type=jnp.float32)
-    part_ref[...] = part
-
-    def share(offset):
+    part_ref[0] = part
+
+    chips = group_size // 2
+    pair = pltpu.make_async_remote_copy(
+        src_ref=part_ref.at[0], dst_ref=part_ref.at[1], send_sem=part_send.at[0], recv_sem=part_recv.at[chips],
+        device_id=(partners[CORE],), device_id_type=MESH)
+    pair.start()
+    pair.wait_recv()
+    chip_part = part + part_ref[1]
+    part_ref[2] = chip_part
+
+    def share(offset, slot):
         return pltpu.make_async_remote_copy(
-            src_ref=part_ref, dst_ref=parts_ref.at[me], send_sem=part_send.at[offset], recv_sem=part_recv.at[me],
-            device_id=((me + offset) % group_size,), device_id_type=MESH)
-
-    def shared(offset):
-        source = (me + group_size - offset) % group_size
-        return pltpu.make_async_remote_copy(
-            src_ref=part_ref, dst_ref=parts_ref.at[source], send_sem=part_send.at[offset], recv_sem=part_recv.at[source],
-            device_id=((me + offset) % group_size,), device_id_type=MESH)
-
-    for offset in range(1, group_size):
-        share(offset).start()
+            src_ref=part_ref.at[2, pl.ds(0, 1)], dst_ref=parts_ref.at[slot, pl.ds(0, 1)], send_sem=part_send.at[offset], recv_sem=part_recv.at[slot],
+            device_id=((me + 2 * offset) % group_size,), device_id_type=MESH)
+
+    for offset in range(1, chips):
+        share(offset, me // 2).start()
     for link in range(CORE):
         swap_back(link, len(SWAP_BLOCKS) - 1).start()
-    parts_ref[me] = part
+    parts_ref[me // 2] = chip_part
+    pair.wait_send()
     for swap in range(len(SWAP_BLOCKS)):
         for link in range(CORE):
             copy = swap_back(link, swap)
             copy.wait_recv()
             out_ref[(QUARTERS - 1 + link) % 4, SWAP_BLOCKS[swap], half_rows(1 - own_bits[link]), :] = back_ref[link, swap]
             copy.wait_send()
-    for offset in range(1, group_size):
-        shared(offset).wait_recv()
-    for offset in range(1, group_size):
-        share(offset).wait_send()
+    for offset in range(1, chips):
+        share(offset, (me // 2 + chips - offset) % chips).wait_recv()
+    for offset in range(1, chips):
+        share(offset, me // 2).wait_send()
 
 
 def flush_kernel(scale, state_ref, parts_ref, out_ref, z_hbm, z_ref, sem, z_sem):
@@ -369,8 +373,8 @@
             copies.append(pltpu.make_async_copy(state_ref.at[quarter, span], out_ref.at[quarter, span], sem.at[quarter, piece]))
     for copy in copies:
         copy.start()
-    total = functools.reduce(jnp.add, [parts_ref[pos] for pos in range(parts_ref.shape[0])])
-    z_ref[...] = total[0:1, :z_ref.shape[1]] * scale
+    total = functools.reduce(jnp.add, [parts_ref[pos, 0:1, :] for pos in range(parts_ref.shape[0])])
+    z_ref[...] = total[:, :z_ref.shape[1]] * scale
     copies.append(pltpu.make_async_copy(z_ref, z_hbm, z_sem))
     copies[-1].start()
     for copy in copies:
@@ -388,7 +392,7 @@
         grid = state_local.reshape(2, row_count, LANES).transpose(1, 0, 2).reshape(shape)
         state, parts = pl.pallas_call(
             functools.partial(kernel, group_size),
-            out_shape=(pltpu.VMEM(shape, jnp.float32), pltpu.VMEM((group_size, 8, LANES), jnp.float32)),
+            out_shape=(pltpu.VMEM(shape, jnp.float32), pltpu.VMEM((group_size // 2, 8, LANES), jnp.float32)),
             in_specs=[pl.BlockSpec(memory_space=pl.ANY)] * 3,
             out_specs=(pl.BlockSpec(memory_space=pltpu.VMEM), pl.BlockSpec(memory_space=pltpu.VMEM)),
             scratch_shapes=[
@@ -399,7 +403,7 @@
                 pltpu.VMEM((HALF, LANES), jnp.float32),
                 pltpu.VMEM((HI_BITS + 1, 8, LANES), jnp.float32),
                 pltpu.VMEM((TOP_BITS, 8, LANES), jnp.float32),
-                pltpu.VMEM((8, LANES), jnp.float32),
+                pltpu.VMEM((3, 8, LANES), jnp.float32),
                 pltpu.SMEM((2, 2, 2, num_qubits), jnp.float32),
                 pltpu.SMEM((2, cz_pairs.shape[0]), jnp.int32),
                 pltpu.SMEM((cz_pairs.shape[0],), jnp.int32),

time: 374 us -> 374 us (level)
  no operation moved by 1% of the time
where the time goes in v4:
time: 374 us
  Pallas kernels  373 us (100%)
    pallas_call x1, Pallas kernels, local_layer(): pl.pallas_call(functools.partial(kernel, group_size), out_shape=(pltpu.VM...  367 us

profile of v4, /device:TPU:0, one launch (start us, length us, event | category | flops | bytes accessed | tf_op | source)
XLA Modules:
  0.0 373.9 jit_solution(13970444924470620243)
XLA Ops:
  0.6 367.1 %shard_map.50 = (f32[4,32,256,128]{3,2,1,0:T(8,128)S(1)}, f32[8,8,128]{2,1,0:T(8,128)S(1)}) custom-call(f32[4,32,256,128]{3,2,1,0:T(8,128)} %bitcast.13, f32[2,2,2,25]{3,2,1,0:T(2,128)} %bitcast.14, s32[2,12]{1,0:T(2,128)} %bitcast.15), custom_call_target="tpu_custom_call" | custom-call | tf_op jit(solution)/shard_map/pallas_call | solution.py:393
  367.8 6.0 %shard_map.51 = (f32[4,32,256,128]{3,2,1,0:T(8,128)}, f32[1,25]{1,0:T(1,128)}) custom-call(f32[4,32,256,128]{3,2,1,0:T(8,128)S(1)} %get-tuple-element.6.state_ref, f32[8,8,128]{2,1,0:T(8,128)S(1)} %get-tuple-element.7.parts_ref), custom_call_target="tpu_custom_call" | custom-call | tf_op jit(solution)/shard_map/pallas_call | solution.py:421

commit v5 on v4

--- a/solution.py
+++ b/solution.py
@@ -17,8 +17,8 @@
 HALF = BLOCK_ROWS // 2
 LOCAL_BLOCKS = 2
 LOAD_SPANS = (1, 6, 9, 16)
-LINK_SPANS = ((1, 6, 9, 16), (16, 16), (16, 16), (16, 10, 3))
-SWAP_BLOCKS = (29, 30, 31)
+LINK_SPANS = ((1, 6, 9, 16), (16, 16), (16, 16), (16, 9, 3))
+SWAP_BLOCKS = (28, 29, 30, 31)
 CORE_SPANS = (8, 8, 8, 8)
 MAX_PIECES = 4
 FLUSH_PIECES = 1
@@ -348,16 +348,25 @@
 
     for offset in range(1, chips):
         share(offset, me // 2).start()
-    for link in range(CORE):
-        swap_back(link, len(SWAP_BLOCKS) - 1).start()
     parts_ref[me // 2] = chip_part
-    pair.wait_send()
-    for swap in range(len(SWAP_BLOCKS)):
+
+    def send_last():
+        for link in range(CORE):
+            swap_back(link, len(SWAP_BLOCKS) - 1).start()
+
+    def take_back(swap):
         for link in range(CORE):
             copy = swap_back(link, swap)
             copy.wait_recv()
             out_ref[(QUARTERS - 1 + link) % 4, SWAP_BLOCKS[swap], half_rows(1 - own_bits[link]), :] = back_ref[link, swap]
             copy.wait_send()
+
+    pl.when(own_bits[CORE] == 0)(send_last)
+    for swap in range(len(SWAP_BLOCKS) - 1):
+        take_back(swap)
+    pl.when(own_bits[CORE] != 0)(send_last)
+    take_back(len(SWAP_BLOCKS) - 1)
+    pair.wait_send()
     for offset in range(1, chips):
         share(offset, (me // 2 + chips - offset) % chips).wait_recv()
     for offset in range(1, chips):

time: 374 us -> 374 us (level)
  no operation moved by 1% of the time
where the time goes in v5:
time: 374 us
  Pallas kernels  373 us (100%)
    pallas_call x1, Pallas kernels, local_layer(): pl.pallas_call(functools.partial(kernel, group_size), out_shape=(pltpu.VM...  367 us

profile of v5, /device:TPU:0, one launch (start us, length us, event | category | flops | bytes accessed | tf_op | source)
XLA Modules:
  0.0 373.6 jit_solution(2646042623752965610)
XLA Ops:
  0.6 366.9 %shard_map.50 = (f32[4,32,256,128]{3,2,1,0:T(8,128)S(1)}, f32[8,8,128]{2,1,0:T(8,128)S(1)}) custom-call(f32[4,32,256,128]{3,2,1,0:T(8,128)} %bitcast.13, f32[2,2,2,25]{3,2,1,0:T(2,128)} %bitcast.14, s32[2,12]{1,0:T(2,128)} %bitcast.15), custom_call_target="tpu_custom_call" | custom-call | tf_op jit(solution)/shard_map/pallas_call | solution.py:402
  367.5 6.0 %shard_map.51 = (f32[4,32,256,128]{3,2,1,0:T(8,128)}, f32[1,25]{1,0:T(1,128)}) custom-call(f32[4,32,256,128]{3,2,1,0:T(8,128)S(1)} %get-tuple-element.6.state_ref, f32[8,8,128]{2,1,0:T(8,128)S(1)} %get-tuple-element.7.parts_ref), custom_call_target="tpu_custom_call" | custom-call | tf_op jit(solution)/shard_map/pallas_call | solution.py:430

commit v6 on v5

--- a/solution.py
+++ b/solution.py
@@ -16,8 +16,8 @@
 BLOCK_ROWS = 2 * 2 ** ROW_BITS
 HALF = BLOCK_ROWS // 2
 LOCAL_BLOCKS = 2
-LOAD_SPANS = (1, 6, 9, 16)
-LINK_SPANS = ((1, 6, 9, 16), (16, 16), (16, 16), (16, 9, 3))
+LOAD_SPANS = (1, 7, 24)
+LINK_SPANS = ((1, 7, 24), (8, 24), (8, 24), (8, 17, 3))
 SWAP_BLOCKS = (28, 29, 30, 31)
 CORE_SPANS = (8, 8, 8, 8)
 MAX_PIECES = 4

time: 374 us -> 374 us (level)
  no operation moved by 1% of the time
where the time goes in v6:
time: 374 us
  Pallas kernels  373 us (100%)
    pallas_call x1, Pallas kernels, local_layer(): pl.pallas_call(functools.partial(kernel, group_size), out_shape=(pltpu.VM...  367 us

profile of v6, /device:TPU:0, one launch (start us, length us, event | category | flops | bytes accessed | tf_op | source)
XLA Modules:
  0.0 373.6 jit_solution(16041124866721472950)
XLA Ops:
  0.6 366.9 %shard_map.50 = (f32[4,32,256,128]{3,2,1,0:T(8,128)S(1)}, f32[8,8,128]{2,1,0:T(8,128)S(1)}) custom-call(f32[4,32,256,128]{3,2,1,0:T(8,128)} %bitcast.13, f32[2,2,2,25]{3,2,1,0:T(2,128)} %bitcast.14, s32[2,12]{1,0:T(2,128)} %bitcast.15), custom_call_target="tpu_custom_call" | custom-call | tf_op jit(solution)/shard_map/pallas_call | solution.py:402
  367.5 6.0 %shard_map.51 = (f32[4,32,256,128]{3,2,1,0:T(8,128)}, f32[1,25]{1,0:T(1,128)}) custom-call(f32[4,32,256,128]{3,2,1,0:T(8,128)S(1)} %get-tuple-element.6.state_ref, f32[8,8,128]{2,1,0:T(8,128)S(1)} %get-tuple-element.7.parts_ref), custom_call_target="tpu_custom_call" | custom-call | tf_op jit(solution)/shard_map/pallas_call | solution.py:430
